TPU v7x, 32 devices: a whole 2x2x4 slice. The times are simulated.
32 devices in a mesh: pipe: 2 (over core), tensor: 2 (over x), expert: 8 (over z, y).
Axes of the slice: x: 2, y: 2, z: 4, core: 2. Of those that a mesh axis runs over, the one named last changes fastest.
Arguments:
- tokens: bfloat16 [3, 384, 4096], P(None, 'expert', 'tensor'), may hold values from -36 to 36
- norm_gain: float32 [2, 4096], P('pipe'), may hold values from 0.1 to 1.9
- shared_gate: bfloat16 [2, 4096, 1024], P('pipe', 'expert', 'tensor'), may hold values from -0.09375 to 0.09375
- shared_up: bfloat16 [2, 4096, 1024], P('pipe', 'expert', 'tensor'), may hold values from -0.09375 to 0.09375
- shared_down: bfloat16 [2, 1024, 4096], P('pipe', 'tensor', 'expert'), may hold values from -0.1875 to 0.1875
- expert_gate: bfloat16 [2, 8, 4096, 1024], P('pipe', 'expert', None, 'tensor'), may hold values from -0.09375 to 0.09375
- expert_up: bfloat16 [2, 8, 4096, 1024], P('pipe', 'expert', None, 'tensor'), may hold values from -0.09375 to 0.09375
- expert_down: bfloat16 [2, 8, 1024, 4096], P('pipe', 'expert', 'tensor'), may hold values from -0.1875 to 0.1875
- expert_ids: int32 [2, 3, 384, 8], P('pipe', None, 'expert'), may hold values from 0 to 255, as said below
- expert_slots: int32 [2, 3, 384, 8], P('pipe', None, 'expert'), may hold values from -1 to 2, as said below
- route_weights: float32 [2, 3, 384, 8], P('pipe', None, 'expert'), may hold values from 0.1 to 1
Outputs:
- states: bfloat16 [2, 3, 384, 4096], P('pipe', None, 'expert', 'tensor')
Inputs may be any that keep to these rules, and one draw needn't show every extreme that they name: `expert_ids`: the 8 ids of a token are distinct. Ids of 8 and above name experts that are not held and add nothing. `expert_slots`: for a choice whose id is below 8: the number of earlier choices (earlier tokens, or lower k of the same token) of the same block of 48 tokens, same layer and microbatch, that name the same expert, if that number is below 3; otherwise -1. For ids of 8 and above: -1.
All inputs are finite; a program needn't handle non-finite values.
Results may differ from a plain program's by a relative error of at most 0.0085.
Values may be sent and summed in bfloat16 or wider, within the bound.
A program may use at most 64 MiB of HBM per device.

v0:
```python
import functools

import jax
import jax.numpy as jnp
from jax import lax
from jax.experimental import pallas as pl
from jax.experimental.pallas import tpu as pltpu
from jax.sharding import PartitionSpec as P

CAP = 3
GATE_PIECES = 2
DOWN_PIECES = 1
EARLY = (0.15, 0.24, 0.45)
EXPERT_END = 0.88
LAST = 0.9
MESH = pl.DeviceIdType.MESH
F32 = jnp.float32
BF16 = jnp.bfloat16


def product(left, right):
    return jnp.dot(left, right, preferred_element_type=F32)


def silu(value):
    return value / (1.0 + jnp.exp(-value))


def layer_kernel(
    ne, nt,
    x_hbm, gain, picker, combine, sg_hbm, su_hbm, sd_hbm, eg_hbm, eu_hbm, ed_hbm,
    out,
    xs, xn, sg, su, sd, eg, eu, ed,
    outg, arr, outc, ret, hy, hr, g_acc, u_acc, hid, eg_acc, eu_acc, ehid, y, rs, res,
    w_send, w_recv, d_send, d_recv, x_send, x_recv, a_send, a_recv, b_send, b_recv,
    f_send, f_recv, h_send, h_recv, r_send, r_recv, p_send, p_recv, own_sem, exp_sem, x_sem, go_sem,
):
    pipe = lax.axis_index("pipe")
    ten = lax.axis_index("tensor")
    me = lax.axis_index("expert")
    spt = ne // nt
    T, Ds = xs.shape[1], xs.shape[2]
    F = sg.shape[2]
    rows = outg.shape[1]
    half = F // 2
    base = ten * spt

    odd = me % 2
    pos = (1 - odd) * (me // 2) + odd * (ne - 1 - me // 2)

    def at(p):
        p = (p + 2 * ne) % ne
        upper = p // (ne // 2)
        return (1 - upper) * (2 * p) + upper * (2 * (ne - 1 - p) + 1)

    def remote(src, dst, send, recv, **device):
        return pltpu.make_async_remote_copy(
            src_ref=src, dst_ref=dst, send_sem=send, recv_sem=recv,
            device_id=device, device_id_type=MESH,
        )

    barrier = pltpu.get_barrier_semaphore()
    for k in range(1, ne):
        pl.semaphore_signal(barrier, inc=1, device_id={"expert": (me + k) % ne}, device_id_type=MESH)
    for k in range(1, nt):
        pl.semaphore_signal(barrier, inc=1, device_id={"tensor": (ten + k) % nt}, device_id_type=MESH)
    pl.semaphore_signal(barrier, inc=1, device_id={"pipe": 1 - pipe}, device_id_type=MESH)

    own = [
        pltpu.make_async_copy(sg_hbm, sg.at[me], own_sem.at[0]),
        pltpu.make_async_copy(su_hbm, su.at[me], own_sem.at[1]),
        pltpu.make_async_copy(sd_hbm, sd.at[me], own_sem.at[2]),
    ]
    for copy in own:
        copy.start()
    x_in = [
        pltpu.make_async_copy(x_hbm.at[:, pl.ds(i * Ds, Ds)], xs.at[base + i], x_sem.at[i])
        for i in range(spt)
    ]

    @pl.when(pipe == 0)
    def _():
        for copy in x_in:
            copy.start()

    experts = [
        pltpu.make_async_copy(eg_hbm, eg, exp_sem.at[0]),
        pltpu.make_async_copy(eu_hbm, eu, exp_sem.at[1]),
        pltpu.make_async_copy(ed_hbm, ed, exp_sem.at[2]),
    ]
    for copy in experts:
        copy.start()
    pl.semaphore_wait(barrier, ne - 1 + nt - 1 + 1)

    right, left = at(pos + 1), at(pos - 1)

    gate_rows, down_rows = Ds // GATE_PIECES, half // DOWN_PIECES

    def gate_copy(s, p):
        block = sg.at[at(pos - s), pl.ds(p * gate_rows, gate_rows)]
        return remote(block, block, w_send.at[0, s, p], w_recv.at[0, s, p], expert=right)

    def up_copy(s, p):
        block = su.at[at(pos + s), pl.ds(p * gate_rows, gate_rows)]
        return remote(block, block, w_send.at[1, s, p], w_recv.at[1, s, p], expert=left)

    def down_a(s, p):
        block = sd.at[at(pos - s), pl.ds(p * down_rows, down_rows)]
        return remote(block, block, d_send.at[0, s, p], d_recv.at[0, s, p], expert=right)

    def down_b(s, p):
        block = sd.at[at(pos + s), pl.ds(half + p * down_rows, down_rows)]
        return remote(block, block, d_send.at[1, s, p], d_recv.at[1, s, p], expert=left)

    pieces = [(make, p) for p in range(GATE_PIECES) for make in (gate_copy, up_copy)]
    pieces += [(make, p) for p in range(DOWN_PIECES) for make in (down_a, down_b)]
    events = [(s, make, p) for s in range(ne - 1) for make, p in pieces]

    def ring(begin, end):
        for s, make, p in events[int(begin * len(events)):int(end * len(events))]:
            make(s, p).wait_recv()
            if s + 1 < ne - 1:
                make(s + 1, p).start()

    @pl.when(pipe == 1)
    def _():
        pl.semaphore_wait(go_sem, 1)

    for copy in own:
        copy.wait()
    for make, p in pieces:
        make(0, p).start()

    @pl.when(pipe == 0)
    def _():
        for copy in x_in:
            copy.wait()

    @pl.when(pipe == 1)
    def _():
        ring(0.0, EARLY[-1])
        for i in range(spt):
            block = xs.at[base + i]
            remote(block, block, p_send.at[i], p_recv.at[i], pipe=1 - pipe).wait_recv()

    def x_copy(k, i):
        block = xs.at[base + i]
        return remote(block, block, x_send.at[k - 1, i], x_recv.at[k - 1, i], tensor=(ten + k) % nt)

    for k in range(1, nt):
        for i in range(spt):
            x_copy(k, i).start()

    @pl.when(pipe == 0)
    def _():
        ring(0.0, EARLY[0])

    for k in range(1, nt):
        for i in range(spt):
            x_copy(k, i).wait_recv()

    def squares(j, total):
        v = xs[j].astype(F32)
        return total + jnp.sum(v * v, axis=-1, keepdims=True)

    total = lax.fori_loop(0, ne, squares, jnp.zeros((T, 1), F32))
    inverse = lax.rsqrt(total / (ne * Ds) + 1e-06)

    def column(i):
        return pl.ds(pl.multiple_of(i * Ds, 128), Ds)

    def normed(j):
        v = (xs[j].astype(F32) * inverse * gain[j]).astype(BF16)
        xn[j] = v
        return v

    def normalise_own(i, carry):
        sent = product(picker[...], normed(base + i)).astype(BF16)
        outg[:, :, column(i)] = sent.reshape(ne, rows, Ds)
        return carry

    lax.fori_loop(0, spt, normalise_own, 0)

    def dispatch(k):
        to = (me + k) % ne
        return remote(outg.at[to], arr.at[ten, me], a_send.at[k - 1], a_recv.at[k - 1], expert=to)

    def spread(q, k):
        block = arr.at[ten, (me + ne - k) % ne]
        return remote(block, block, f_send.at[q - 1, k], f_recv.at[q - 1, k], tensor=(ten + q) % nt)

    def give_back(k):
        to = (me + k) % ne
        return remote(outc.at[to], ret.at[me], b_send.at[k - 1], b_recv.at[k - 1], expert=to)

    for k in range(1, ne):
        dispatch(k).start()
    arr[ten, me] = outg[me]
    for q in range(1, nt):
        spread(q, 0).start()

    @pl.when(pipe == 0)
    def _():
        ring(EARLY[0], EARLY[1])

    def normalise_others(j, carry):
        normed((base + spt + j) % ne)
        return carry

    lax.fori_loop(0, ne - spt, normalise_others, 0)
    g_acc[...] = product(xn[me], sg[me])
    u_acc[...] = product(xn[me], su[me])

    def shared(s):
        a, b = at(pos - s - 1), at(pos + s + 1)
        g_acc[...] += product(xn[a], sg[a])
        u_acc[...] += product(xn[b], su[b])

    @pl.when(pipe == 0)
    def _():
        ring(EARLY[1], EARLY[2])

    for copy in experts:
        copy.wait()
    for k in range(1, ne):
        dispatch(k).wait_recv()
        for q in range(1, nt):
            spread(q, k).start()
    ticks = [EARLY[2]]

    def tick():
        later = ticks[0] + (EXPERT_END - EARLY[2]) / (4 * ne)
        ring(ticks[0], later)
        ticks[0] = later

    eg_acc[...] = jnp.zeros_like(eg_acc)
    eu_acc[...] = jnp.zeros_like(eu_acc)

    def expert_in(group):
        for i in range(spt):
            depth = pl.ds(pl.multiple_of(group * (spt * Ds) + i * Ds, 128), Ds)
            v = arr[group, :, :, i * Ds:(i + 1) * Ds].reshape(ne * rows, Ds)
            eg_acc[...] += product(v, eg[depth, :])
            tick()
            eu_acc[...] += product(v, eu[depth, :])
            tick()

    expert_in(ten)
    for q in range(1, nt):
        for k in range(ne):
            spread(q, k).wait_recv()
        expert_in((ten + q) % nt)
    ehid[...] = (silu(eg_acc[...]) * eu_acc[...]).astype(BF16)

    def h_copy(q, i):
        slot = (q - 1) * spt + i
        return remote(hy.at[slot], hr.at[slot], h_send.at[slot], h_recv.at[slot], tensor=(ten + q) % nt)

    def expert_out(group, i):
        return product(ehid[...], ed[:, pl.ds(pl.multiple_of(group * (spt * Ds) + i * Ds, 128), Ds)])

    for q in range(1, nt):
        for i in range(spt):
            hy[(q - 1) * spt + i] = expert_out((ten + q) % nt, i).astype(BF16)
            h_copy(q, i).start()
            tick()
            tick()
    for i in range(spt):
        value = expert_out(ten, i)
        for q in range(1, nt):
            h_copy(q, i).wait_recv()
            value += hr[(q - 1) * spt + i].astype(F32)
        outc[:, :, i * Ds:(i + 1) * Ds] = value.astype(BF16).reshape(ne, rows, Ds)
        tick()
        tick()
    for k in range(1, ne):
        give_back(k).start()
    ret[me] = outc[me]
    held = ticks[0]
    for s in range(ne - 2):
        later = max(held, min(held + (LAST - held) * (s + 1) / (ne - 3), (s + 2) / (ne - 1), 1.0))
        if s == ne - 3:
            @pl.when(pipe == 0)
            def _():
                pl.semaphore_signal(go_sem, inc=1, device_id={"pipe": 1 - pipe}, device_id_type=MESH)

            later = 1.0
        ring(held, max(held, (s + 1) / (ne - 1)))
        held = max(held, (s + 1) / (ne - 1))
        shared(s)
        ring(held, max(held, later))
        held = max(held, later)
    shared(ne - 2)
    hid[...] = (silu(g_acc[...]) * u_acc[...]).astype(BF16)

    def terms(j):
        return product(hid[...], sd[j])

    def r_copy(k, i):
        to = (ten + k) % nt
        slot = (k - 1) * spt + i
        return remote(y.at[slot], rs.at[slot], r_send.at[slot], r_recv.at[slot], tensor=to)

    for k in range(1, nt):
        for i in range(spt):
            y[(k - 1) * spt + i] = terms(((ten + k) % nt) * spt + i).astype(BF16)
            r_copy(k, i).start()

    for k in range(1, ne):
        give_back(k).wait_recv()
    weights = combine[...]
    high = weights.astype(BF16)
    low = (weights - high.astype(F32)).astype(BF16)
    for i in range(spt):
        v = ret[:, :, i * Ds:(i + 1) * Ds].reshape(ne * rows, Ds)
        value = xs[base + i].astype(F32) + terms(base + i) + (product(high, v) + product(low, v))
        for k in range(1, nt):
            r_copy(k, i).wait_recv()
            value += rs[(k - 1) * spt + i].astype(F32)
        value = value.astype(BF16)
        res[i] = value
        out[:, i * Ds:(i + 1) * Ds] = value

        @pl.when(pipe == 0)
        def _():
            remote(res.at[i], xs.at[base + i], p_send.at[i], p_recv.at[i], pipe=1 - pipe).start()

    for s in range(ne - 1):
        for make, p in pieces:
            make(s, p).wait_send()
    for k in range(1, ne):
        dispatch(k).wait_send()
        give_back(k).wait_send()
    for k in range(1, nt):
        for i in range(spt):
            x_copy(k, i).wait_send()
            r_copy(k, i).wait_send()
            h_copy(k, i).wait_send()
        for i in range(ne):
            spread(k, i).wait_send()

    @pl.when(pipe == 0)
    def _():
        for i in range(spt):
            remote(res.at[i], xs.at[base + i], p_send.at[i], p_recv.at[i], pipe=1 - pipe).wait_send()


def per_device(
    tokens, norm_gain, shared_gate, shared_up, shared_down,
    expert_gate, expert_up, expert_down, expert_ids, expert_slots, route_weights,
):
    ne = lax.axis_size("expert")
    nt = lax.axis_size("tensor")
    batches, block, width = tokens.shape
    T = batches * block
    D = width * nt
    Ds = shared_gate.shape[1]
    F = shared_gate.shape[2]
    FE = expert_gate.shape[3]
    spt = ne // nt
    rows = -(-batches * CAP // 16) * 16

    ids, slots, weights = expert_ids[0], expert_slots[0], route_weights[0]
    valid = (ids < ne) & (slots >= 0)
    batch = jnp.arange(batches, dtype=jnp.int32)[:, None, None]
    code = jnp.where(valid, ids * rows + batch * CAP + slots, -1).reshape(T, -1)
    matched = code[:, :, None] == jnp.arange(ne * rows, dtype=jnp.int32)[None, None, :]
    picker = jnp.any(matched, axis=1).T.astype(BF16)
    combine = jnp.sum(jnp.where(matched, weights.reshape(T, -1)[:, :, None], F32(0.0)), axis=1)

    vmem = pl.BlockSpec(memory_space=pltpu.VMEM)
    hbm = pl.BlockSpec(memory_space=pl.ANY)
    dma = pltpu.SemaphoreType.DMA
    steps = ne - 1
    others = max(nt - 1, 1)
    out = pl.pallas_call(
        functools.partial(layer_kernel, ne, nt),
        out_shape=jax.ShapeDtypeStruct((T, width), BF16),
        in_specs=[hbm, vmem, vmem, vmem] + [hbm] * 6,
        out_specs=vmem,
        scratch_shapes=[
            pltpu.VMEM((ne, T, Ds), BF16),
            pltpu.VMEM((ne, T, Ds), BF16),
            pltpu.VMEM((ne, Ds, F), BF16),
            pltpu.VMEM((ne, Ds, F), BF16),
            pltpu.VMEM((ne, F, Ds), BF16),
            pltpu.VMEM((D, FE), BF16),
            pltpu.VMEM((D, FE), BF16),
            pltpu.VMEM((FE, D), BF16),
            pltpu.VMEM((ne, rows, width), BF16),
            pltpu.VMEM((nt, ne, rows, width), BF16),
            pltpu.VMEM((ne, rows, width), BF16),
            pltpu.VMEM((ne, rows, width), BF16),
            pltpu.VMEM((others * spt, ne * rows, Ds), BF16),
            pltpu.VMEM((others * spt, ne * rows, Ds), BF16),
            pltpu.VMEM((T, F), F32),
            pltpu.VMEM((T, F), F32),
            pltpu.VMEM((T, F), BF16),
            pltpu.VMEM((ne * rows, FE), F32),
            pltpu.VMEM((ne * rows, FE), F32),
            pltpu.VMEM((ne * rows, FE), BF16),
            pltpu.VMEM((others * spt, T, Ds), BF16),
            pltpu.VMEM((others * spt, T, Ds), BF16),
            pltpu.VMEM((spt, T, Ds), BF16),
            dma((2, steps, GATE_PIECES)), dma((2, steps, GATE_PIECES)),
            dma((2, steps, DOWN_PIECES)), dma((2, steps, DOWN_PIECES)),
            dma((others, spt)), dma((others, spt)),
            dma((steps,)), dma((steps,)), dma((steps,)), dma((steps,)),
            dma((others, ne)), dma((others, ne)),
            dma((others * spt,)), dma((others * spt,)),
            dma((others * spt,)), dma((others * spt,)),
            dma((spt,)), dma((spt,)),
            dma((3,)), dma((3,)), dma((spt,)),
            pltpu.SemaphoreType.REGULAR,
        ],
        compiler_params=pltpu.CompilerParams(
            collective_id=0, has_side_effects=True, vmem_limit_bytes=60 * 1024 * 1024
        ),
    )(
        tokens.reshape(T, width), norm_gain[0].reshape(ne, 1, Ds), picker, combine,
        shared_gate[0], shared_up[0], shared_down[0],
        expert_gate[0, 0], expert_up[0, 0], expert_down[0, 0],
    )
    return out.reshape(1, batches, block, width)


def solution(mesh):
    in_specs = (
        P(None, "expert", "tensor"),
        P("pipe", None),
        P("pipe", "expert", "tensor"),
        P("pipe", "expert", "tensor"),
        P("pipe", "tensor", "expert"),
        P("pipe", "expert", None, "tensor"),
        P("pipe", "expert", None, "tensor"),
        P("pipe", "expert", "tensor", None),
        P("pipe", None, "expert", None),
        P("pipe", None, "expert", None),
        P("pipe", None, "expert", None),
    )
    out_specs = P("pipe", None, "expert", "tensor")
    return jax.shard_map(
        per_device, mesh=mesh, in_specs=in_specs, out_specs=out_specs, check_vma=False
    )
```

profile of v0, /device:TPU:7, one launch (start us, length us, event | category | flops | bytes accessed | tf_op | source)
XLA Modules:
  0.0 165.7 jit_solution(9441655410457279137)
XLA Ops:
  0.0 0.1 add.23
  0.1 0.1 add.24
  0.2 0.7 broadcast_compare_fusion
  0.9 0.1 lt.15
  1.0 0.7 broadcast_multiply_fusion
  1.7 0.1 mul.23
  1.8 0.7 copy.26
  2.5 0.1 squeeze.22
  2.6 0.1 copy.28
  2.7 0.3 fusion
  3.0 0.7 copy.29
  3.7 0.8 copy.32
  4.5 1.0 select_reduce_fusion.combine
  5.5 158.2 %shard_map.109 = bf16[144,2048]{1,0:T(8,128)(2,1)} custom-call(bf16[144,2048]{1,0:T(8,128)(2,1)} %bitcast.21, f32[8,1,512]{2,1,0:T(1,128)} %bitcast.27, bf16[128,144]{1,0:T(8,128)(2,1)} %bitcast.26, f32[144,128]{1,0:T(8,128)} %select_reduce_fusion.combine, bf16[512,512]{1,0:T(8,128)(2,1)} %bitcast.22, bf16[512,512]{1,0:T(8,128)(2,1)} %bitcast.23, ...), custom_call_target="tpu_custom_call" | custom-call | tf_op jit(solution)/shard_map/pallas_call | solution.py:376
  163.8 1.9 %copy.35 = bf16[1,3,48,2048]{3,2,1,0:T(8,128)(2,1)} copy(bf16[1,3,48,2048]{3,2,1,0:T(8,128)(2,1)} %bitcast.20) | data formatting | bytes 1179648
  (5 shorter events, 0.0 us)
where the time goes:
time: 166 us
  Pallas kernels  158 us (95%)
  local copies, waits for them, and re-layouts  4.68 us (3%)
  other arithmetic  2.75 us (2%)
    pallas_call x1, Pallas kernels, per_device(): pl.pallas_call(functools.partial(layer_kernel, ne, nt), out_shape=jax.Sha...  158 us

commit v1 on v0

v1 whole, which is shorter than its diff:
```python
import functools

import jax
import jax.numpy as jnp
from jax import lax
from jax.experimental import pallas as pl
from jax.experimental.pallas import tpu as pltpu
from jax.sharding import PartitionSpec as P

CAP = 3
GROUP = 2
MESH = pl.DeviceIdType.MESH
F32 = jnp.float32
BF16 = jnp.bfloat16


def product(left, right):
    return jnp.dot(left, right, preferred_element_type=F32)


def silu(value):
    return value / (1.0 + jnp.exp(-value))


def layer_kernel(
    ne, nt, ng,
    x_hbm, gain, picker, combine, sg_hbm, su_hbm, sd_hbm, eg_hbm, eu_hbm, ed_hbm,
    out,
    xs, xr, sq, sqn, inv, xn, xg, sg, su, sd, eg, eu, ed,
    gs, gr, own_acc, hid, oy, oz,
    outg, arr, outc, ret, hy, hr, eg_acc, eu_acc, ehid, res,
    wx_send, wx_recv, wy_send, wy_recv, fx_send, fx_recv, fy_send, fy_recv,
    q_send, q_recv, q2_send, x_send, x_recv, p_send, p_recv, p2_send,
    s_send, s_recv, g_send, g_recv, n_send, n_recv, o_send, o_recv,
    a_send, a_recv, b_send, b_recv, f_send, f_recv, h_send, h_recv,
    own_sem, exp_sem, x_sem, go_sem,
):
    pipe = lax.axis_index("pipe")
    ten = lax.axis_index("tensor")
    me = lax.axis_index("expert")
    no = ne // ng
    spt = ne // nt
    opt = spt // ng
    grp = me // ng
    sub = me % ng
    T, Gs = xs.shape[1], xs.shape[2]
    R = xr.shape[1]
    step = (T - R) // max(nt - 1, 1)
    Ds, F = sg.shape[2], sg.shape[3]
    FS = nt * F
    rows = outg.shape[1]
    width = opt * Gs
    owner = grp // opt
    slot = grp % opt

    def remote(src, dst, send, recv, **device):
        return pltpu.make_async_remote_copy(
            src_ref=src, dst_ref=dst, send_sem=send, recv_sem=recv,
            device_id=device, device_id_type=MESH,
        )

    def far(d):
        return (grp + d) % no

    def expert_at(group):
        return group * ng + sub

    def tensor_at(k):
        return (ten + k) % nt

    def subset(k):
        return pl.ds(pl.multiple_of(k * step, 16), R)

    barrier = pltpu.get_barrier_semaphore()
    greeted = 0
    for k in range(1, ne):
        pl.semaphore_signal(barrier, inc=1, device_id={"expert": (me + k) % ne}, device_id_type=MESH)
        greeted += 1
    for k in range(1, nt):
        pl.semaphore_signal(barrier, inc=1, device_id={"tensor": tensor_at(k)}, device_id_type=MESH)
        greeted += 1
        for d in range(1, no):
            pl.semaphore_signal(
                barrier, inc=1, device_id={"tensor": tensor_at(k), "expert": expert_at(far(d))}, device_id_type=MESH
            )
            greeted += 1
    for k in range(nt):
        pl.semaphore_signal(
            barrier, inc=1, device_id={"pipe": 1 - pipe, "tensor": tensor_at(k)}, device_id_type=MESH
        )
        greeted += 1

    x_in = [
        pltpu.make_async_copy(x_hbm.at[:, pl.ds(i * Gs, Gs)], xs.at[i], x_sem.at[i])
        for i in range(opt)
    ]

    @pl.when(pipe == 0)
    def _():
        for copy in x_in:
            copy.start()

    own = [
        pltpu.make_async_copy(sg_hbm, sg.at[ten, sub], own_sem.at[0]),
        pltpu.make_async_copy(su_hbm, su.at[ten, sub], own_sem.at[1]),
        pltpu.make_async_copy(sd_hbm, sd.at[sub, ten], own_sem.at[2]),
    ]
    for copy in own:
        copy.start()
    experts = [
        pltpu.make_async_copy(eg_hbm, eg, exp_sem.at[0]),
        pltpu.make_async_copy(eu_hbm, eu, exp_sem.at[1]),
        pltpu.make_async_copy(ed_hbm, ed, exp_sem.at[2]),
    ]
    for copy in experts:
        copy.start()
    pl.semaphore_wait(barrier, greeted)

    def shard(w, t, j):
        if w == 2:
            return sd.at[j, t]
        return (sg, su)[w].at[t, j]

    cut = (Ds // 2, Ds // 2, F // 2)
    full = (Ds, Ds, F)

    def weight_x(w, k):
        block = shard(w, ten, sub)
        return remote(block, block, wx_send.at[w, k - 1], wx_recv.at[w, k - 1], tensor=tensor_at(k))

    def weight_y(w, r):
        block = shard(w, ten, sub)
        return remote(block, block, wy_send.at[w, r - 1], wy_recv.at[w, r - 1], expert=grp * ng + (sub + r) % ng)

    def forward_y(w, k, r):
        block = shard(w, (ten + nt - k) % nt, sub).at[pl.ds(0, cut[w])]
        return remote(
            block, block, fy_send.at[w, k - 1, r - 1], fy_recv.at[w, k - 1, r - 1],
            expert=grp * ng + (sub + r) % ng,
        )

    def forward_x(w, k, r):
        block = shard(w, ten, (sub + ng - r) % ng).at[pl.ds(cut[w], full[w] - cut[w])]
        return remote(
            block, block, fx_send.at[w, k - 1, r - 1], fx_recv.at[w, k - 1, r - 1], tensor=tensor_at(k)
        )

    def send_x(w):
        for k in range(1, nt):
            weight_x(w, k).start()

    def send_y(w):
        for r in range(1, ng):
            weight_y(w, r).start()

    def pass_x(w):
        for r in range(1, ng):
            weight_y(w, r).wait_recv()
            for k in range(1, nt):
                forward_x(w, k, r).start()

    def pass_y(w):
        for k in range(1, nt):
            weight_x(w, k).wait_recv()
            for r in range(1, ng):
                forward_y(w, k, r).start()

    def gathered(w):
        for k in range(1, nt):
            for r in range(1, ng):
                forward_x(w, k, r).wait_recv()
                forward_y(w, k, r).wait_recv()

    first = pipe == 0

    @pl.when(pipe == 1)
    def _():
        pl.semaphore_wait(go_sem, 1)

    def x_copy(k, i):
        return remote(
            xs.at[i, subset(tensor_at(k))], xr.at[ten * opt + i],
            x_send.at[k - 1, i], x_recv.at[k - 1, i], tensor=tensor_at(k),
        )

    def q_copy(k):
        return remote(sq.at[ten], sq.at[ten], q_send.at[k], q_recv.at[k], tensor=tensor_at(k))

    def squares(total):
        return jnp.broadcast_to(total, (T, sq.shape[2]))

    @pl.when(first)
    def _():
        total = jnp.zeros((T, 1), F32)
        for i in range(opt):
            x_in[i].wait()
            for k in range(1, nt):
                x_copy(k, i).start()
            v = xs[i].astype(F32)
            total += jnp.sum(v * v, axis=-1, keepdims=True)
        sq[ten] = squares(total)
        for k in range(1, nt):
            q_copy(k).start()

    for copy in own:
        copy.wait()

    @pl.when(first)
    def _():
        send_x(0)
        send_y(0)
        send_y(1)

    @pl.when(pipe == 1)
    def _():
        for w in range(3):
            send_x(w)
            send_y(w)
        for w in range(3):
            pass_x(w)
            pass_y(w)
        for w in range(3):
            gathered(w)
        for i in range(opt):
            remote(xs.at[i], xs.at[i], p_send.at[i], p_recv.at[i], pipe=1 - pipe).wait_recv()
        q_copy(0).wait_recv()

    for k in range(1, nt):
        q_copy(k).wait_recv()
    total = sq[0]
    for t in range(1, nt):
        total += sq[t]
    inv[...] = lax.rsqrt(total / (ne * Ds) + 1e-06)

    def spread_rows(o):
        return remote(xn.at[o], xg.at[grp], s_send.at[o], s_recv.at[grp], expert=expert_at(o))

    mine = inv[subset(ten), :1]

    def normed_rows(o, value):
        xn[o] = (value.astype(F32) * mine * gain[o]).astype(BF16)

        @pl.when(o != grp)
        def _():
            spread_rows(o).start()

    for i in range(opt):
        normed_rows(ten * opt + i, xs[i, subset(ten)])
    for k in range(1, nt):
        for i in range(opt):
            x_copy(k, i).wait_recv()
            o = ((ten + nt - k) % nt) * opt + i
            normed_rows(o, xr[o])

    def dispatch(k):
        to = (me + k) % ne
        return remote(outg.at[to], arr.at[ten, me], a_send.at[k - 1], a_recv.at[k - 1], expert=to)

    def spread(q, k):
        block = arr.at[ten, (me + ne - k) % ne]
        return remote(block, block, f_send.at[q - 1, k], f_recv.at[q - 1, k], tensor=tensor_at(q))

    def give_back(k):
        to = (me + k) % ne
        return remote(outc.at[to], ret.at[me], b_send.at[k - 1], b_recv.at[k - 1], expert=to)

    for i in range(opt):
        v = (xs[i].astype(F32) * inv[:, :1] * gain[ten * opt + i]).astype(BF16)
        for c in range(ng):
            sent = product(picker[...], v[:, c * Ds:(c + 1) * Ds]).astype(BF16)
            outg[:, :, i * Gs + c * Ds:i * Gs + (c + 1) * Ds] = sent.reshape(ne, rows, Ds)
    for k in range(1, ne):
        dispatch(k).start()
    arr[ten, me] = outg[me]

    @pl.when(first)
    def _():
        pass_x(0)
        send_x(1)
        pass_y(0)
        pass_x(1)
        gathered(0)

    def await_group(sem, o, ref):
        remote(ref, ref, sem, sem, expert=expert_at(o)).wait_recv()

    def partial(w, o):
        return remote(gs.at[w, o], gr.at[w, grp], g_send.at[w, o], g_recv.at[w, grp], expert=expert_at(o))

    def partials(w):
        weights = (sg, su)[w]
        for d in range(1, no):
            o = far(d)
            if w == 0:
                await_group(s_recv.at[o], o, xg.at[o])
            for t in range(nt):
                gs[w, o, :, t * F:(t + 1) * F] = product(xg[o], weights[t].reshape(Gs, F)).astype(BF16)
            partial(w, o).start()

    def own_partials(w):
        weights = (sg, su)[w]
        for t in range(nt):
            own_acc[w, :, t * F:(t + 1) * F] = product(xn[grp], weights[t].reshape(Gs, F))

    partials(0)

    @pl.when(first)
    def _():
        pass_y(1)
        gathered(1)

    partials(1)
    for q in range(1, nt):
        spread(q, 0).start()
    for k in range(1, ne):
        dispatch(k).wait_recv()
        for q in range(1, nt):
            spread(q, k).start()

    @pl.when(first)
    def _():
        send_x(2)
        send_y(2)

    own_partials(0)
    own_partials(1)

    for copy in experts:
        copy.wait()
    eg_acc[...] = jnp.zeros_like(eg_acc)
    eu_acc[...] = jnp.zeros_like(eu_acc)

    def expert_in(group):
        for i in range(spt):
            depth = pl.ds(pl.multiple_of(group * (spt * Ds) + i * Ds, 128), Ds)
            v = arr[group, :, :, i * Ds:(i + 1) * Ds].reshape(ne * rows, Ds)
            eg_acc[...] += product(v, eg[depth, :])
            eu_acc[...] += product(v, eu[depth, :])

    expert_in(ten)
    for q in range(1, nt):
        for k in range(ne):
            spread(q, k).wait_recv()
        expert_in((ten + q) % nt)
    ehid[...] = (silu(eg_acc[...]) * eu_acc[...]).astype(BF16)

    def h_copy(q, i):
        at = (q - 1) * spt + i
        return remote(hy.at[at], hr.at[at], h_send.at[at], h_recv.at[at], tensor=tensor_at(q))

    def expert_out(group, i):
        return product(ehid[...], ed[:, pl.ds(pl.multiple_of(group * (spt * Ds) + i * Ds, 128), Ds)])

    for q in range(1, nt):
        for i in range(spt):
            hy[(q - 1) * spt + i] = expert_out((ten + q) % nt, i).astype(BF16)
            h_copy(q, i).start()

    def hidden(o):
        return remote(hid.at[grp], hid.at[grp], n_send.at[o], n_recv.at[grp], expert=expert_at(o))

    for w in range(2):
        for d in range(1, no):
            o = far(d)
            await_group(g_recv.at[w, o], o, gr.at[w, o])
    g, u = own_acc[0], own_acc[1]
    for d in range(1, no):
        o = far(d)
        g += gr[0, o].astype(F32)
        u += gr[1, o].astype(F32)
    hid[grp] = (silu(g) * u).astype(BF16)
    for d in range(1, no):
        hidden(far(d)).start()

    @pl.when(first)
    def _():
        pass_x(2)
        pass_y(2)
        pl.semaphore_signal(go_sem, inc=1, device_id={"pipe": 1 - pipe}, device_id_type=MESH)

    for i in range(spt):
        value = expert_out(ten, i)
        for q in range(1, nt):
            h_copy(q, i).wait_recv()
            value += hr[(q - 1) * spt + i].astype(F32)
        outc[:, :, i * Ds:(i + 1) * Ds] = value.astype(BF16).reshape(ne, rows, Ds)
    for k in range(1, ne):
        give_back(k).start()
    ret[me] = outc[me]

    @pl.when(first)
    def _():
        gathered(2)

    def o_copy(o):
        return remote(
            oy.at[o], oz.at[slot, ten], o_send.at[o], o_recv.at[slot, ten], tensor=owner, expert=expert_at(o)
        )

    for d in list(range(1, no)) + [0]:
        o = far(d)
        if d > 0:
            await_group(n_recv.at[o], o, hid.at[o])
        for j in range(ng):
            oy[o, :, j * Ds:(j + 1) * Ds] = product(hid[o], sd[j].reshape(FS, Ds)).astype(BF16)
        if d > 0:
            o_copy(o).start()
        else:
            @pl.when(owner != ten)
            def _():
                o_copy(o).start()

            @pl.when(owner == ten)
            def _():
                oz[slot, ten] = oy[o]

    weights = combine[...]
    high = weights.astype(BF16)
    low = (weights - high.astype(F32)).astype(BF16)
    for k in range(1, ne):
        give_back(k).wait_recv()

    def raw_on(k, i):
        return remote(
            res.at[i, subset(tensor_at(k))], xr.at[ten * opt + i], p2_send.at[k - 1, i], x_recv.at[k - 1, i],
            pipe=1 - pipe, tensor=tensor_at(k),
        )

    def state_on(i):
        return remote(res.at[i], xs.at[i], p_send.at[i], p_recv.at[i], pipe=1 - pipe)

    def squares_on(k):
        return remote(sqn, sq.at[ten], q2_send.at[k], q_recv.at[k], pipe=1 - pipe, tensor=tensor_at(k))

    total = jnp.zeros((T, 1), F32)
    for i in range(opt):
        for s in range(nt):
            @pl.when((ten * opt + i != grp) | (s != ten))
            def _():
                remote(
                    oz.at[i, s], oz.at[i, s], o_recv.at[i, s], o_recv.at[i, s], tensor=(ten + 1) % nt
                ).wait_recv()

        v = ret[:, :, i * Gs:(i + 1) * Gs].reshape(ne * rows, Gs)
        value = xs[i].astype(F32) + (product(high, v) + product(low, v))
        value += jnp.concatenate(
            [oz[i, s, :(step if s + 1 < nt else T - s * step)] for s in range(nt)], axis=0
        ).astype(F32)
        value = value.astype(BF16)
        res[i] = value
        out[:, i * Gs:(i + 1) * Gs] = value

        @pl.when(first)
        def _():
            for k in range(1, nt):
                raw_on(k, i).start()
            state_on(i).start()

        wide = value.astype(F32)
        total += jnp.sum(wide * wide, axis=-1, keepdims=True)

    @pl.when(first)
    def _():
        sqn[...] = squares(total)
        for k in range(nt):
            squares_on(k).start()

    for w in range(3):
        for k in range(1, nt):
            weight_x(w, k).wait_send()
        for r in range(1, ng):
            weight_y(w, r).wait_send()
        for k in range(1, nt):
            for r in range(1, ng):
                forward_x(w, k, r).wait_send()
                forward_y(w, k, r).wait_send()
    for d in range(1, no):
        o = far(d)
        spread_rows(o).wait_send()
        partial(0, o).wait_send()
        partial(1, o).wait_send()
        hidden(o).wait_send()
        o_copy(o).wait_send()

    @pl.when(owner != ten)
    def _():
        o_copy(grp).wait_send()

    for k in range(1, ne):
        dispatch(k).wait_send()
        give_back(k).wait_send()
    for q in range(1, nt):
        for i in range(spt):
            h_copy(q, i).wait_send()
        for k in range(ne):
            spread(q, k).wait_send()

    @pl.when(first)
    def _():
        for k in range(1, nt):
            q_copy(k).wait_send()
            for i in range(opt):
                x_copy(k, i).wait_send()
                raw_on(k, i).wait_send()
        for i in range(opt):
            state_on(i).wait_send()
        for k in range(nt):
            squares_on(k).wait_send()


def per_device(
    tokens, norm_gain, shared_gate, shared_up, shared_down,
    expert_gate, expert_up, expert_down, expert_ids, expert_slots, route_weights,
):
    ne = lax.axis_size("expert")
    nt = lax.axis_size("tensor")
    batches, block, width = tokens.shape
    T = batches * block
    D = width * nt
    Ds = shared_gate.shape[1]
    F = shared_gate.shape[2]
    FE = expert_gate.shape[3]
    spt = ne // nt
    ng = GROUP
    no = ne // ng
    opt = spt // ng
    Gs = ng * Ds
    FS = nt * F
    step = T // nt // 16 * 16
    R = T - (nt - 1) * step
    rows = -(-batches * CAP // 16) * 16

    ids, slots, weights = expert_ids[0], expert_slots[0], route_weights[0]
    valid = (ids < ne) & (slots >= 0)
    batch = jnp.arange(batches, dtype=jnp.int32)[:, None, None]
    code = jnp.where(valid, ids * rows + batch * CAP + slots, -1).reshape(T, -1)
    matched = code[:, :, None] == jnp.arange(ne * rows, dtype=jnp.int32)[None, None, :]
    picker = jnp.any(matched, axis=1).T.astype(BF16)
    combine = jnp.sum(jnp.where(matched, weights.reshape(T, -1)[:, :, None], F32(0.0)), axis=1)

    vmem = pl.BlockSpec(memory_space=pltpu.VMEM)
    hbm = pl.BlockSpec(memory_space=pl.ANY)
    dma = pltpu.SemaphoreType.DMA
    others = max(nt - 1, 1)
    near = max(ng - 1, 1)
    out = pl.pallas_call(
        functools.partial(layer_kernel, ne, nt, ng),
        out_shape=jax.ShapeDtypeStruct((T, width), BF16),
        in_specs=[hbm, vmem, vmem, vmem] + [hbm] * 6,
        out_specs=vmem,
        scratch_shapes=[
            pltpu.VMEM((opt, T, Gs), BF16),
            pltpu.VMEM((no, R, Gs), BF16),
            pltpu.VMEM((nt, T, 128), F32),
            pltpu.VMEM((T, 128), F32),
            pltpu.VMEM((T, 128), F32),
            pltpu.VMEM((no, R, Gs), BF16),
            pltpu.VMEM((no, R, Gs), BF16),
            pltpu.VMEM((nt, ng, Ds, F), BF16),
            pltpu.VMEM((nt, ng, Ds, F), BF16),
            pltpu.VMEM((ng, nt, F, Ds), BF16),
            pltpu.VMEM((D, FE), BF16),
            pltpu.VMEM((D, FE), BF16),
            pltpu.VMEM((FE, D), BF16),
            pltpu.VMEM((2, no, R, FS), BF16),
            pltpu.VMEM((2, no, R, FS), BF16),
            pltpu.VMEM((2, R, FS), F32),
            pltpu.VMEM((no, R, FS), BF16),
            pltpu.VMEM((no, R, Gs), BF16),
            pltpu.VMEM((opt, nt, R, Gs), BF16),
            pltpu.VMEM((ne, rows, width), BF16),
            pltpu.VMEM((nt, ne, rows, width), BF16),
            pltpu.VMEM((ne, rows, width), BF16),
            pltpu.VMEM((ne, rows, width), BF16),
            pltpu.VMEM((others * spt, ne * rows, Ds), BF16),
            pltpu.VMEM((others * spt, ne * rows, Ds), BF16),
            pltpu.VMEM((ne * rows, FE), F32),
            pltpu.VMEM((ne * rows, FE), F32),
            pltpu.VMEM((ne * rows, FE), BF16),
            pltpu.VMEM((opt, T, Gs), BF16),
            dma((3, others)), dma((3, others)), dma((3, near)), dma((3, near)),
            dma((3, others, near)), dma((3, others, near)), dma((3, others, near)), dma((3, others, near)),
            dma((nt,)), dma((nt,)), dma((nt,)),
            dma((others, opt)), dma((others, opt)), dma((opt,)), dma((opt,)), dma((others, opt)),
            dma((no,)), dma((no,)), dma((2, no)), dma((2, no)),
            dma((no,)), dma((no,)), dma((no,)), dma((opt, nt)),
            dma((ne - 1,)), dma((ne - 1,)), dma((ne - 1,)), dma((ne - 1,)),
            dma((others, ne)), dma((others, ne)),
            dma((others * spt,)), dma((others * spt,)),
            dma((3,)), dma((3,)), dma((opt,)),
            pltpu.SemaphoreType.REGULAR,
        ],
        compiler_params=pltpu.CompilerParams(
            collective_id=0, has_side_effects=True, vmem_limit_bytes=60 * 1024 * 1024
        ),
    )(
        tokens.reshape(T, width), norm_gain[0].reshape(no, 1, Gs), picker, combine,
        shared_gate[0], shared_up[0], shared_down[0],
        expert_gate[0, 0], expert_up[0, 0], expert_down[0, 0],
    )
    return out.reshape(1, batches, block, width)


def solution(mesh):
    in_specs = (
        P(None, "expert", "tensor"),
        P("pipe", None),
        P("pipe", "expert", "tensor"),
        P("pipe", "expert", "tensor"),
        P("pipe", "tensor", "expert"),
        P("pipe", "expert", None, "tensor"),
        P("pipe", "expert", None, "tensor"),
        P("pipe", "expert", "tensor", None),
        P("pipe", None, "expert", None),
        P("pipe", None, "expert", None),
        P("pipe", None, "expert", None),
    )
    out_specs = P("pipe", None, "expert", "tensor")
    return jax.shard_map(
        per_device, mesh=mesh, in_specs=in_specs, out_specs=out_specs, check_vma=False
    )
```

time: 166 us -> 149 us (0.90); the launches traced: 166 us -> 147 us
  Pallas kernels: 158 us -> 140 us
    pallas_call x1, Pallas kernels: 158 us -> 140 us  [per_device(): pl.pallas_call(functools.partial(layer_kernel, ne, nt, ng), out_shape=jax...]
where the time goes in v1:
time: 149 us; the launch traced here: 147 us
  Pallas kernels  140 us (94%)
  local copies, waits for them, and re-layouts  4.68 us (3%)
  other arithmetic  2.75 us (2%)
    pallas_call x1, Pallas kernels, per_device(): pl.pallas_call(functools.partial(layer_kernel, ne, nt, ng), out_shape=jax...  140 us

profile of v1, /device:TPU:7, one launch (start us, length us, event | category | flops | bytes accessed | tf_op | source)
XLA Modules:
  0.0 147.0 jit_solution(9831264412038100171)
XLA Ops:
  0.0 0.1 add.23
  0.1 0.1 add.24
  0.2 0.7 broadcast_compare_fusion
  0.9 0.1 lt.15
  1.0 0.7 broadcast_multiply_fusion
  1.7 0.1 mul.23
  1.8 0.7 copy.26
  2.5 0.1 squeeze.22
  2.6 0.1 copy.28
  2.7 0.3 fusion
  3.0 0.7 copy.29
  3.7 0.8 copy.32
  4.5 1.0 select_reduce_fusion.combine
  5.5 139.5 %shard_map.109 = bf16[144,2048]{1,0:T(8,128)(2,1)} custom-call(bf16[144,2048]{1,0:T(8,128)(2,1)} %bitcast.21, f32[4,1,1024]{2,1,0:T(1,128)} %bitcast.27, bf16[128,144]{1,0:T(8,128)(2,1)} %bitcast.26, f32[144,128]{1,0:T(8,128)} %select_reduce_fusion.combine, bf16[512,512]{1,0:T(8,128)(2,1)} %bitcast.22, bf16[512,512]{1,0:T(8,128)(2,1)} %bitcast.23, ...), custom_call_target="tpu_custom_call" | custom-call | tf_op jit(solution)/shard_map/pallas_call | solution.py:546
  145.1 1.9 %copy.35 = bf16[1,3,48,2048]{3,2,1,0:T(8,128)(2,1)} copy(bf16[1,3,48,2048]{3,2,1,0:T(8,128)(2,1)} %bitcast.20) | data formatting | bytes 1179648
  (5 shorter events, 0.0 us)

commit v2 on v1

--- a/solution.py
+++ b/solution.py
@@ -9,6 +9,7 @@
 
 CAP = 3
 GROUP = 2
+PACK = 8
 MESH = pl.DeviceIdType.MESH
 F32 = jnp.float32
 BF16 = jnp.bfloat16
@@ -18,17 +19,22 @@
     return jnp.dot(left, right, preferred_element_type=F32)
 
 
+def turned(left, right):
+    return lax.dot_general(left, right, (((0,), (0,)), ((), ())), preferred_element_type=F32)
+
+
 def silu(value):
     return value / (1.0 + jnp.exp(-value))
 
 
 def layer_kernel(
     ne, nt, ng,
-    x_hbm, gain, picker, combine, sg_hbm, su_hbm, sd_hbm, eg_hbm, eu_hbm, ed_hbm,
+    x_hbm, gain, ids, slots, shares, sg_hbm, su_hbm, sd_hbm, eg_hbm, eu_hbm, ed_hbm,
     out,
     xs, xr, sq, sqn, inv, xn, xg, sg, su, sd, eg, eu, ed,
     gs, gr, own_acc, hid, oy, oz,
-    outg, arr, outc, ret, hy, hr, eg_acc, eu_acc, ehid, res,
+    pick_low, pick_high, pick_tail, comb_high, comb_low,
+    outg, arr, outc, ret, er, rt, tails, hy, hr, eg_acc, eu_acc, ehid, res,
     wx_send, wx_recv, wy_send, wy_recv, fx_send, fx_recv, fy_send, fy_recv,
     q_send, q_recv, q2_send, x_send, x_recv, p_send, p_recv, p2_send,
     s_send, s_recv, g_send, g_recv, n_send, n_recv, o_send, o_recv,
@@ -48,8 +54,13 @@
     step = (T - R) // max(nt - 1, 1)
     Ds, F = sg.shape[2], sg.shape[3]
     FS = nt * F
-    rows = outg.shape[1]
     width = opt * Gs
+    half = spt // 2
+    wide = half * Ds
+    lanes = tails.shape[1]
+    chunks = Ds // lanes
+    kept = rt.shape[0]
+    batches, top, block = ids.shape
     owner = grp // opt
     slot = grp % opt
 
@@ -64,6 +75,9 @@
 
     def expert_at(group):
         return group * ng + sub
+
+    def beside(r):
+        return grp * ng + (sub + r) % ng
 
     def tensor_at(k):
         return (ten + k) % nt
@@ -124,58 +138,61 @@
     cut = (Ds // 2, Ds // 2, F // 2)
     full = (Ds, Ds, F)
 
-    def weight_x(w, k):
-        block = shard(w, ten, sub)
-        return remote(block, block, wx_send.at[w, k - 1], wx_recv.at[w, k - 1], tensor=tensor_at(k))
-
-    def weight_y(w, r):
-        block = shard(w, ten, sub)
-        return remote(block, block, wy_send.at[w, r - 1], wy_recv.at[w, r - 1], expert=grp * ng + (sub + r) % ng)
+    def piece(w, t, j, p):
+        return shard(w, t, j).at[pl.ds(p * cut[w], cut[w] if p == 0 else full[w] - cut[w])]
+
+    def weight_x(w, k, p):
+        block = piece(w, ten, sub, p)
+        return remote(block, block, wx_send.at[w, k - 1, p], wx_recv.at[w, k - 1, p], tensor=tensor_at(k))
+
+    def weight_y(w, r, p):
+        block = piece(w, ten, sub, p)
+        return remote(block, block, wy_send.at[w, r - 1, p], wy_recv.at[w, r - 1, p], expert=beside(r))
 
     def forward_y(w, k, r):
-        block = shard(w, (ten + nt - k) % nt, sub).at[pl.ds(0, cut[w])]
+        block = piece(w, (ten + nt - k) % nt, sub, 0)
         return remote(
-            block, block, fy_send.at[w, k - 1, r - 1], fy_recv.at[w, k - 1, r - 1],
-            expert=grp * ng + (sub + r) % ng,
+            block, block, fy_send.at[w, k - 1, r - 1], fy_recv.at[w, k - 1, r - 1], expert=beside(r)
         )
 
     def forward_x(w, k, r):
-        block = shard(w, ten, (sub + ng - r) % ng).at[pl.ds(cut[w], full[w] - cut[w])]
+        block = piece(w, ten, (sub + ng - r) % ng, 1)
         return remote(
             block, block, fx_send.at[w, k - 1, r - 1], fx_recv.at[w, k - 1, r - 1], tensor=tensor_at(k)
         )
 
     def send_x(w):
-        for k in range(1, nt):
-            weight_x(w, k).start()
-
-    def send_y(w):
+        for p in range(2):
+            for k in range(1, nt):
+                weight_x(w, k, p).start()
+
+    def send_y(w, p):
         for r in range(1, ng):
-            weight_y(w, r).start()
+            weight_y(w, r, p).start()
 
     def pass_x(w):
         for r in range(1, ng):
-            weight_y(w, r).wait_recv()
+            weight_y(w, r, 1).wait_recv()
             for k in range(1, nt):
                 forward_x(w, k, r).start()
 
     def pass_y(w):
         for k in range(1, nt):
-            weight_x(w, k).wait_recv()
+            weight_x(w, k, 0).wait_recv()
             for r in range(1, ng):
                 forward_y(w, k, r).start()
 
     def gathered(w):
+        for k in range(1, nt):
+            weight_x(w, k, 1).wait_recv()
+        for r in range(1, ng):
+            weight_y(w, r, 0).wait_recv()
         for k in range(1, nt):
             for r in range(1, ng):
                 forward_x(w, k, r).wait_recv()
                 forward_y(w, k, r).wait_recv()
 
     first = pipe == 0
-
-    @pl.when(pipe == 1)
-    def _():
-        pl.semaphore_wait(go_sem, 1)
 
     def x_copy(k, i):
         return remote(
@@ -194,13 +211,14 @@
         total = jnp.zeros((T, 1), F32)
         for i in range(opt):
             x_in[i].wait()
-            for k in range(1, nt):
-                x_copy(k, i).start()
             v = xs[i].astype(F32)
             total += jnp.sum(v * v, axis=-1, keepdims=True)
         sq[ten] = squares(total)
         for k in range(1, nt):
             q_copy(k).start()
+        for k in range(1, nt):
+            for i in range(opt):
+                x_copy(k, i).start()
 
     for copy in own:
         copy.wait()
@@ -208,18 +226,50 @@
     @pl.when(first)
     def _():
         send_x(0)
-        send_y(0)
-        send_y(1)
+        send_y(0, 1)
+        send_y(0, 0)
+        send_y(1, 1)
+
+    def rows_like(count):
+        return lax.broadcasted_iota(jnp.int32, (count, block), 0)
+
+    def marked(count, code, value):
+        total = jnp.zeros((count, block), F32)
+        for k in range(top):
+            total = jnp.where(rows_like(count) == code[k:k + 1], value(k), total)
+        return total
+
+    for m in range(batches):
+        held = (ids[m] < ne) & (slots[m] >= 0)
+        place = slots[m] + m * CAP
+        code = jnp.where(held & (place < PACK), ids[m] * (2 * PACK) + place, -2 * PACK)
+        tail = jnp.where(held & (place >= PACK), ids[m], -1)
+        back = jnp.where(place < PACK, ids[m] * PACK + place, ne * PACK + ids[m])
+        back = jnp.where(held, back, -1)
+        pick_low[m] = marked(pick_low.shape[1], code, lambda k: 1.0).astype(BF16)
+        pick_high[m] = marked(pick_high.shape[1], code + PACK, lambda k: 1.0).astype(BF16)
+        pick_tail[m] = marked(pick_tail.shape[1], tail, lambda k: 1.0).astype(BF16)
+        share = marked(kept, back, lambda k: shares[m, k:k + 1, :])
+        high = share.astype(BF16)
+        comb_high[m] = high
+        comb_low[m] = (share - high.astype(F32)).astype(BF16)
 
     @pl.when(pipe == 1)
     def _():
-        for w in range(3):
+        pl.semaphore_wait(go_sem.at[0], 1)
+        for w in range(2):
+            send_y(w, 1)
+            send_y(w, 0)
+        pl.semaphore_wait(go_sem.at[1], 1)
+        for w in range(2):
             send_x(w)
-            send_y(w)
-        for w in range(3):
+        for w in range(2):
             pass_x(w)
             pass_y(w)
-        for w in range(3):
+        send_x(2)
+        send_y(2, 1)
+        send_y(2, 0)
+        for w in range(2):
             gathered(w)
         for i in range(opt):
             remote(xs.at[i], xs.at[i], p_send.at[i], p_recv.at[i], pipe=1 - pipe).wait_recv()
@@ -264,11 +314,44 @@
         to = (me + k) % ne
         return remote(outc.at[to], ret.at[me], b_send.at[k - 1], b_recv.at[k - 1], expert=to)
 
-    for i in range(opt):
-        v = (xs[i].astype(F32) * inv[:, :1] * gain[ten * opt + i]).astype(BF16)
-        for c in range(ng):
-            sent = product(picker[...], v[:, c * Ds:(c + 1) * Ds]).astype(BF16)
-            outg[:, :, i * Gs + c * Ds:i * Gs + (c + 1) * Ds] = sent.reshape(ne, rows, Ds)
+    def own_normed(c):
+        i, at = c * Ds // Gs, c * Ds % Gs
+        column = gain[ten * opt + i]
+        return (xs[i, :, at:at + Ds].astype(F32) * inv[:, :1] * column[:, at:at + Ds]).astype(BF16)
+
+    def put_tail(c, value):
+        for j in range(chunks):
+            tails[pl.ds(c * chunks + j, ne, stride=2 * PACK), :] = value[:, j * lanes:(j + 1) * lanes]
+
+    def packed_tails():
+        return tails[...].reshape(ne, 2 * PACK, lanes).astype(BF16)
+
+    def unpack(read, put):
+        for c in range(half):
+            both = read(c * Ds, Ds).astype(F32)
+            put(0, ne * PACK, c * Ds, both[:, :PACK].reshape(ne * PACK, Ds))
+            put(0, ne * PACK, wide + c * Ds, both[:, PACK:].reshape(ne * PACK, Ds))
+        tails[...] = read(wide, lanes).astype(F32).reshape(ne * 2 * PACK, lanes)
+        for c in range(spt * chunks):
+            row = tails[pl.ds(c, ne, stride=2 * PACK), :]
+            if kept > ne * PACK + ne:
+                row = jnp.concatenate([row, jnp.zeros((kept - ne * PACK - ne, lanes), F32)], axis=0)
+            put(ne * PACK, kept, c * lanes, row)
+
+    tails[...] = jnp.zeros_like(tails)
+    for c in range(half):
+        v = (own_normed(c), own_normed(half + c))
+        sent = jnp.zeros((ne * 2 * PACK, Ds), F32)
+        last = [jnp.zeros((pick_tail.shape[1], Ds), F32)] * 2
+        for m in range(batches):
+            token = slice(m * block, (m + 1) * block)
+            sent += product(pick_low[m], v[0][token]) + product(pick_high[m], v[1][token])
+            if (m + 1) * CAP > PACK:
+                last = [last[h] + product(pick_tail[m], v[h][token]) for h in range(2)]
+        outg[:, :, c * Ds:(c + 1) * Ds] = sent.astype(BF16).reshape(ne, 2 * PACK, Ds)
+        for h in range(2):
+            put_tail(h * half + c, last[h][:ne])
+    outg[:, :, wide:] = packed_tails()
     for k in range(1, ne):
         dispatch(k).start()
     arr[ten, me] = outg[me]
@@ -278,6 +361,7 @@
         pass_x(0)
         send_x(1)
         pass_y(0)
+        send_y(1, 0)
         pass_x(1)
         gathered(0)
 
@@ -304,23 +388,29 @@
 
     partials(0)
 
+    def spreading():
+        for q in range(1, nt):
+            spread(q, 0).start()
+        for k in range(1, ne):
+            dispatch(k).wait_recv()
+            for q in range(1, nt):
+                spread(q, k).start()
+
     @pl.when(first)
     def _():
         pass_y(1)
+        spreading()
+        send_x(2)
+        send_y(2, 1)
+        send_y(2, 0)
         gathered(1)
+        pl.semaphore_signal(go_sem.at[0], inc=1, device_id={"pipe": 1 - pipe}, device_id_type=MESH)
 
     partials(1)
-    for q in range(1, nt):
-        spread(q, 0).start()
-    for k in range(1, ne):
-        dispatch(k).wait_recv()
-        for q in range(1, nt):
-            spread(q, k).start()
-
-    @pl.when(first)
-    def _():
-        send_x(2)
-        send_y(2)
+
+    @pl.when(pipe == 1)
+    def _():
+        spreading()
 
     own_partials(0)
     own_partials(1)
@@ -331,13 +421,18 @@
     eu_acc[...] = jnp.zeros_like(eu_acc)
 
     def expert_in(group):
+        def put(begin, end, column, value):
+            er[begin:end, column:column + value.shape[1]] = value.astype(BF16)
+
+        unpack(lambda column, count: arr[group, :, :, column:column + count], put)
         for i in range(spt):
             depth = pl.ds(pl.multiple_of(group * (spt * Ds) + i * Ds, 128), Ds)
-            v = arr[group, :, :, i * Ds:(i + 1) * Ds].reshape(ne * rows, Ds)
+            v = er[:, i * Ds:(i + 1) * Ds]
             eg_acc[...] += product(v, eg[depth, :])
             eu_acc[...] += product(v, eu[depth, :])
 
     expert_in(ten)
+    pass_x(2)
     for q in range(1, nt):
         for k in range(ne):
             spread(q, k).wait_recv()
@@ -355,6 +450,8 @@
         for i in range(spt):
             hy[(q - 1) * spt + i] = expert_out((ten + q) % nt, i).astype(BF16)
             h_copy(q, i).start()
+
+    pass_y(2)
 
     def hidden(o):
         return remote(hid.at[grp], hid.at[grp], n_send.at[o], n_recv.at[grp], expert=expert_at(o))
@@ -372,25 +469,28 @@
     for d in range(1, no):
         hidden(far(d)).start()
 
-    @pl.when(first)
-    def _():
-        pass_x(2)
-        pass_y(2)
-        pl.semaphore_signal(go_sem, inc=1, device_id={"pipe": 1 - pipe}, device_id_type=MESH)
-
-    for i in range(spt):
+    def expert_sum(i):
         value = expert_out(ten, i)
         for q in range(1, nt):
             h_copy(q, i).wait_recv()
             value += hr[(q - 1) * spt + i].astype(F32)
-        outc[:, :, i * Ds:(i + 1) * Ds] = value.astype(BF16).reshape(ne, rows, Ds)
+        put_tail(i, value[ne * PACK:ne * PACK + ne])
+        return value[:ne * PACK].reshape(ne, PACK, Ds)
+
+    tails[...] = jnp.zeros_like(tails)
+    for c in range(half):
+        both = jnp.concatenate([expert_sum(c), expert_sum(half + c)], axis=1)
+        outc[:, :, c * Ds:(c + 1) * Ds] = both.astype(BF16)
+    outc[:, :, wide:] = packed_tails()
     for k in range(1, ne):
         give_back(k).start()
     ret[me] = outc[me]
 
     @pl.when(first)
     def _():
-        gathered(2)
+        pl.semaphore_signal(go_sem.at[1], inc=1, device_id={"pipe": 1 - pipe}, device_id_type=MESH)
+
+    gathered(2)
 
     def o_copy(o):
         return remote(
@@ -414,11 +514,19 @@
             def _():
                 oz[slot, ten] = oy[o]
 
-    weights = combine[...]
-    high = weights.astype(BF16)
-    low = (weights - high.astype(F32)).astype(BF16)
     for k in range(1, ne):
         give_back(k).wait_recv()
+
+    def put_back(begin, end, column, value):
+        rt[begin:end, column:column + value.shape[1]] = value.astype(BF16)
+
+    unpack(lambda column, count: ret[:, :, column:column + count], put_back)
+
+    def routed(i):
+        v = rt[:, i * Gs:(i + 1) * Gs]
+        return jnp.concatenate(
+            [turned(comb_high[m], v) + turned(comb_low[m], v) for m in range(batches)], axis=0
+        )
 
     def raw_on(k, i):
         return remote(
@@ -441,8 +549,7 @@
                     oz.at[i, s], oz.at[i, s], o_recv.at[i, s], o_recv.at[i, s], tensor=(ten + 1) % nt
                 ).wait_recv()
 
-        v = ret[:, :, i * Gs:(i + 1) * Gs].reshape(ne * rows, Gs)
-        value = xs[i].astype(F32) + (product(high, v) + product(low, v))
+        value = xs[i].astype(F32) + routed(i)
         value += jnp.concatenate(
             [oz[i, s, :(step if s + 1 < nt else T - s * step)] for s in range(nt)], axis=0
         ).astype(F32)
@@ -452,24 +559,26 @@
 
         @pl.when(first)
         def _():
-            for k in range(1, nt):
-                raw_on(k, i).start()
             state_on(i).start()
 
-        wide = value.astype(F32)
-        total += jnp.sum(wide * wide, axis=-1, keepdims=True)
+        rounded = value.astype(F32)
+        total += jnp.sum(rounded * rounded, axis=-1, keepdims=True)
 
     @pl.when(first)
     def _():
         sqn[...] = squares(total)
         for k in range(nt):
             squares_on(k).start()
+        for k in range(1, nt):
+            for i in range(opt):
+                raw_on(k, i).start()
 
     for w in range(3):
-        for k in range(1, nt):
-            weight_x(w, k).wait_send()
-        for r in range(1, ng):
-            weight_y(w, r).wait_send()
+        for p in range(2):
+            for k in range(1, nt):
+                weight_x(w, k, p).wait_send()
+            for r in range(1, ng):
+                weight_y(w, r, p).wait_send()
         for k in range(1, nt):
             for r in range(1, ng):
                 forward_x(w, k, r).wait_send()
@@ -515,6 +624,7 @@
     ne = lax.axis_size("expert")
     nt = lax.axis_size("tensor")
     batches, block, width = tokens.shape
+    assert PACK <= batches * CAP <= PACK + 1
     T = batches * block
     D = width * nt
     Ds = shared_gate.shape[1]
@@ -528,15 +638,10 @@
     FS = nt * F
     step = T // nt // 16 * 16
     R = T - (nt - 1) * step
-    rows = -(-batches * CAP // 16) * 16
-
-    ids, slots, weights = expert_ids[0], expert_slots[0], route_weights[0]
-    valid = (ids < ne) & (slots >= 0)
-    batch = jnp.arange(batches, dtype=jnp.int32)[:, None, None]
-    code = jnp.where(valid, ids * rows + batch * CAP + slots, -1).reshape(T, -1)
-    matched = code[:, :, None] == jnp.arange(ne * rows, dtype=jnp.int32)[None, None, :]
-    picker = jnp.any(matched, axis=1).T.astype(BF16)
-    combine = jnp.sum(jnp.where(matched, weights.reshape(T, -1)[:, :, None], F32(0.0)), axis=1)
+    lanes = 128
+    packed = width // 2 + lanes
+    spare = -(-ne // 16) * 16
+    kept = ne * PACK + spare
 
     vmem = pl.BlockSpec(memory_space=pltpu.VMEM)
     hbm = pl.BlockSpec(memory_space=pl.ANY)
@@ -546,7 +651,7 @@
     out = pl.pallas_call(
         functools.partial(layer_kernel, ne, nt, ng),
         out_shape=jax.ShapeDtypeStruct((T, width), BF16),
-        in_specs=[hbm, vmem, vmem, vmem] + [hbm] * 6,
+        in_specs=[hbm, vmem, vmem, vmem, vmem] + [hbm] * 6,
         out_specs=vmem,
         scratch_shapes=[
             pltpu.VMEM((opt, T, Gs), BF16),
@@ -568,17 +673,25 @@
             pltpu.VMEM((no, R, FS), BF16),
             pltpu.VMEM((no, R, Gs), BF16),
             pltpu.VMEM((opt, nt, R, Gs), BF16),
-            pltpu.VMEM((ne, rows, width), BF16),
-            pltpu.VMEM((nt, ne, rows, width), BF16),
-            pltpu.VMEM((ne, rows, width), BF16),
-            pltpu.VMEM((ne, rows, width), BF16),
-            pltpu.VMEM((others * spt, ne * rows, Ds), BF16),
-            pltpu.VMEM((others * spt, ne * rows, Ds), BF16),
-            pltpu.VMEM((ne * rows, FE), F32),
-            pltpu.VMEM((ne * rows, FE), F32),
-            pltpu.VMEM((ne * rows, FE), BF16),
+            pltpu.VMEM((batches, ne * 2 * PACK, block), BF16),
+            pltpu.VMEM((batches, ne * 2 * PACK, block), BF16),
+            pltpu.VMEM((batches, spare, block), BF16),
+            pltpu.VMEM((batches, kept, block), BF16),
+            pltpu.VMEM((batches, kept, block), BF16),
+            pltpu.VMEM((ne, 2 * PACK, packed), BF16),
+            pltpu.VMEM((nt, ne, 2 * PACK, packed), BF16),
+            pltpu.VMEM((ne, 2 * PACK, packed), BF16),
+            pltpu.VMEM((ne, 2 * PACK, packed), BF16),
+            pltpu.VMEM((kept, width), BF16),
+            pltpu.VMEM((kept, width), BF16),
+            pltpu.VMEM((ne * 2 * PACK, lanes), F32),
+            pltpu.VMEM((others * spt, kept, Ds), BF16),
+            pltpu.VMEM((others * spt, kept, Ds), BF16),
+            pltpu.VMEM((kept, FE), F32),
+            pltpu.VMEM((kept, FE), F32),
+            pltpu.VMEM((kept, FE), BF16),
             pltpu.VMEM((opt, T, Gs), BF16),
-            dma((3, others)), dma((3, others)), dma((3, near)), dma((3, near)),
+            dma((3, others, 2)), dma((3, others, 2)), dma((3, near, 2)), dma((3, near, 2)),
             dma((3, others, near)), dma((3, others, near)), dma((3, others, near)), dma((3, others, near)),
             dma((nt,)), dma((nt,)), dma((nt,)),
             dma((others, opt)), dma((others, opt)), dma((opt,)), dma((opt,)), dma((others, opt)),
@@ -588,13 +701,14 @@
             dma((others, ne)), dma((others, ne)),
             dma((others * spt,)), dma((others * spt,)),
             dma((3,)), dma((3,)), dma((opt,)),
-            pltpu.SemaphoreType.REGULAR,
+            pltpu.SemaphoreType.REGULAR((2,)),
         ],
         compiler_params=pltpu.CompilerParams(
             collective_id=0, has_side_effects=True, vmem_limit_bytes=60 * 1024 * 1024
         ),
     )(
-        tokens.reshape(T, width), norm_gain[0].reshape(no, 1, Gs), picker, combine,
+        tokens.reshape(T, width), norm_gain[0].reshape(no, 1, Gs),
+        *(array[0].transpose(0, 2, 1) for array in (expert_ids, expert_slots, route_weights)),
         shared_gate[0], shared_up[0], shared_down[0],
         expert_gate[0, 0], expert_up[0, 0], expert_down[0, 0],
     )

time: 149 us -> 122 us (0.82)
  the two profiles are of different devices: /device:TPU:7 before, /device:TPU:29 now
where the time goes in v2:
time: 122 us
  Pallas kernels  120 us (98%)
  local copies, waits for them, and re-layouts  1.93 us (2%)
    pallas_call x1, Pallas kernels, per_device(): pl.pallas_call(functools.partial(layer_kernel, ne, nt, ng), out_shape=jax...  120 us

profile of v2, /device:TPU:29, one launch (start us, length us, event | category | flops | bytes accessed | tf_op | source)
XLA Modules:
  0.0 121.7 jit_solution(7757744444485791687)
XLA Ops:
  0.0 119.7 %shard_map.109 = bf16[144,2048]{1,0:T(8,128)(2,1)} custom-call(bf16[144,2048]{1,0:T(8,128)(2,1)} %bitcast.22, f32[4,1,1024]{2,1,0:T(1,128)} %bitcast.26, s32[3,8,48]{2,1,0:T(8,128)} %bitcast.27, s32[3,8,48]{2,1,0:T(8,128)} %bitcast.28, f32[3,8,48]{2,1,0:T(8,128)} %bitcast.29, bf16[512,512]{1,0:T(8,128)(2,1)} %bitcast.23, bf16[512,512]{1,0:T(8,128)(2,1)} %bitcast.24, ...), custom_call_target="tpu_custom_call" | custom-call | tf_op jit(solution)/shard_map/pallas_call | solution.py:651
  119.7 1.9 %copy.13 = bf16[1,3,48,2048]{3,2,1,0:T(8,128)(2,1)} copy(bf16[1,3,48,2048]{3,2,1,0:T(8,128)(2,1)} %bitcast.21) | data formatting | bytes 1179648
